TPU v7x, 32 devices: a whole 2x2x4 slice. The times are simulated.
32 devices in a mesh: section: 2 (over x), dp: 16 (over z, y, core).
Axes of the slice: x: 2, y: 2, z: 4, core: 2. Of those that a mesh axis runs over, the one named last changes fastest.
Arguments:
- activations: bfloat16 [2, 8, 768, 5376], P('section', None, 'dp'), may hold values from -6 to 6
- loss_grads: bfloat16 [8, 768, 5376], P(None, 'dp'), may hold values from -6 to 6
- adapter_in: bfloat16 [2, 5376, 64], P('section'), may hold values from -0.078125 to 0.078125
- adapter_out: bfloat16 [2, 64, 5376], P('section'), may hold values from -0.75 to 0.75
- first_moment: float32 [2, 16, 86016], P('section', 'dp'), may hold values from -0.4 to 0.4
- second_moment: float32 [2, 16, 86016], P('section', 'dp'), may hold values from 0.0001 to 0.01
- old_owner: int32 [2, 8], P('section'), may hold values from 0 to 15, as said below
- new_owner: int32 [2, 16], P('section'), may hold values from 0 to 15, each once within a row
- plan: int32 [8], replicated, may hold values from 0 to 7, each once
Outputs:
- input_grads: bfloat16 [2, 8, 768, 5376], P('section', None, 'dp')
- adam_update: float32 [2, 16, 43008], P('section', 'dp')
- first_new: float32 [2, 16, 43008], P('section', 'dp')
- second_new: float32 [2, 16, 43008], P('section', 'dp')
Inputs may be any that keep to these rules, and one draw needn't show every extreme that they name: `old_owner`: the entries of one section's row are distinct.
All inputs are finite; a program needn't handle non-finite values.
Results may differ from a plain program's by a relative error of at most 0.025.
Values may be sent and summed in bfloat16 or wider, within the bound.
A program may use at most 64 MiB of HBM per device.

v0:
```python
import jax
import jax.numpy as jnp
from jax import lax
from jax.sharding import PartitionSpec as P

beta_one = 0.9
beta_two = 0.95
adam_eps = 1e-08
adam_step = 1000.0
loss_scale = 4096.0


def passed_along(value, axis, steps):
    count = lax.axis_size(axis)
    first, last = (max(0, -steps), min(count, count - steps))
    return lax.ppermute(value, axis, [(source, source + steps) for source in range(first, last)])


def silu_slope(pre_value):
    gate_value = jax.nn.sigmoid(pre_value)
    return gate_value * (1.0 + pre_value * (1.0 - gate_value))


def per_device(
    activations,
    loss_grads,
    adapter_in,
    adapter_out,
    first_moment,
    second_moment,
    old_owner,
    new_owner,
    plan,
):
    sections = lax.axis_size("section")
    section_index = lax.axis_index("section")
    replicas = lax.axis_size("dp")
    my_index = lax.axis_index("dp")
    weight_in = adapter_in[0]
    weight_out = adapter_out[0]
    inputs_all = activations[0]
    micro_count = inputs_all.shape[0]
    tok_rows = inputs_all.shape[1]
    width = inputs_all.shape[2]
    owners_old = old_owner[0]
    owners_new = new_owner[0]
    block_len = first_moment.shape[2] // 2
    replica_ids = jnp.arange(replicas, dtype=jnp.int32)
    new_block = jnp.sum(jnp.where(owners_new == my_index, replica_ids, 0))

    def drain_turn(turn_index, state):
        previous, grad_in, grad_out, emitted = state
        received = passed_along(previous, "section", -1)
        slot = turn_index - (sections - 1 - section_index)
        is_valid = (slot >= 0) & (slot < micro_count)
        clamped = jnp.clip(slot, 0, micro_count - 1)
        micro = lax.dynamic_index_in_dim(plan, clamped, 0, keepdims=False)
        section_input = lax.dynamic_index_in_dim(inputs_all, micro, 0, keepdims=False)
        from_loss = lax.dynamic_index_in_dim(loss_grads, micro, 0, keepdims=False)
        incoming = jnp.where(section_index == sections - 1, from_loss, received)
        pre_value = jnp.dot(section_input, weight_in, preferred_element_type=jnp.float32)
        hidden = jax.nn.silu(pre_value).astype(jnp.bfloat16)
        act_grad = jnp.dot(incoming, weight_out.T, preferred_element_type=jnp.float32)
        pre_grad = (act_grad * silu_slope(pre_value)).astype(jnp.bfloat16)
        input_grad = (
            incoming.astype(jnp.float32)
            + jnp.dot(pre_grad, weight_in.T, preferred_element_type=jnp.float32)
        ).astype(jnp.bfloat16)
        valid_weight = is_valid.astype(jnp.float32)
        grad_in = grad_in + valid_weight * jnp.dot(
            section_input.T, pre_grad, preferred_element_type=jnp.float32
        )
        grad_out = grad_out + valid_weight * jnp.dot(
            hidden.T, incoming, preferred_element_type=jnp.float32
        )
        earlier = lax.dynamic_index_in_dim(emitted, clamped, 0, keepdims=False)
        written = jnp.where(is_valid, input_grad, earlier)
        emitted = lax.dynamic_update_index_in_dim(emitted, written, clamped, 0)
        return (input_grad, grad_in, grad_out, emitted)

    start_state = (
        jnp.zeros((tok_rows, width), jnp.bfloat16),
        jnp.zeros(weight_in.shape, jnp.float32),
        jnp.zeros(weight_out.shape, jnp.float32),
        jnp.zeros((micro_count, tok_rows, width), jnp.bfloat16),
    )
    last_grad, grad_in, grad_out, emitted = lax.fori_loop(
        0, micro_count + sections - 1, drain_turn, start_state
    )
    partial_value = jnp.concatenate([grad_in.reshape(-1), grad_out.reshape(-1)])
    totals = lax.psum(partial_value, "dp")
    grads = lax.dynamic_slice_in_dim(totals, new_block * block_len, block_len) / loss_scale
    old_count = owners_old.shape[0]
    piece_len = 2 * block_len // replicas
    first_pieces = first_moment[0, 0].reshape(replicas, piece_len)
    second_pieces = second_moment[0, 0].reshape(replicas, piece_len)
    first_spread = lax.all_to_all(first_pieces, "dp", split_axis=0, concat_axis=0, tiled=True)
    second_spread = lax.all_to_all(second_pieces, "dp", split_axis=0, concat_axis=0, tiled=True)
    first_held = jnp.take(first_spread, owners_old, axis=0)
    second_held = jnp.take(second_spread, owners_old, axis=0)
    my_half = my_index // old_count
    targets = owners_new.reshape(-1, 2)
    target_of_block = jnp.where(my_half == 0, targets[:, 0], targets[:, 1])
    picker = (target_of_block[None, :] == replica_ids[:, None]).astype(jnp.float32)
    first_out = jnp.dot(picker, first_held, precision=lax.Precision.HIGHEST)
    second_out = jnp.dot(picker, second_held, precision=lax.Precision.HIGHEST)
    first_got = lax.all_to_all(first_out, "dp", split_axis=0, concat_axis=0, tiled=True)
    second_got = lax.all_to_all(second_out, "dp", split_axis=0, concat_axis=0, tiled=True)
    half_start = new_block % 2 * old_count
    first_mine = lax.dynamic_slice_in_dim(first_got, half_start, old_count, 0).reshape(-1)
    second_mine = lax.dynamic_slice_in_dim(second_got, half_start, old_count, 0).reshape(-1)
    moved = (first_mine, second_mine)
    first_old, second_old = moved
    first_next = beta_one * first_old + (1.0 - beta_one) * grads
    second_next = beta_two * second_old + (1.0 - beta_two) * grads * grads
    update = (
        first_next
        / (1.0 - beta_one**adam_step)
        / (jnp.sqrt(second_next / (1.0 - beta_two**adam_step)) + adam_eps)
    )
    return (emitted[None], update[None, None], first_next[None, None], second_next[None, None])


def solution(mesh):
    placed = (
        P("section", None, "dp", None),
        P(None, "dp", None),
        P("section", None, None),
        P("section", None, None),
        P("section", "dp", None),
        P("section", "dp", None),
        P("section", None),
        P("section", None),
        P(),
    )
    return jax.shard_map(
        per_device,
        mesh=mesh,
        in_specs=placed,
        out_specs=(
            P("section", None, "dp", None),
            P("section", "dp", None),
            P("section", "dp", None),
            P("section", "dp", None),
        ),
        check_vma=False,
    )
```

profile of v0, /device:TPU:0, one launch (start us, length us, event | category | flops | bytes accessed | tf_op | source)
XLA Modules:
  0.0 360.3 jit_solution(12223333010346438085)
XLA Ops:
  7.2 7.6 %all-to-all-start.2 = ((f32[16,1,5376]{2,1,0:T(1,128)}), f32[16,1,5376]{2,1,0:T(1,128)S(1)}, u32[]{:S(2)}, u32[]{:S(2)}) async-start(f32[16,1,5376]{2,1,0:T(1,128)} %bitcast.84), calls=%async_computation.2 | async-start | bytes 688128 | tf_op jit(solution)/shard_map/all_to_all | solution.py:98
  17.8 8.3 %all-to-all-done.2 = f32[16,1,5376]{2,1,0:T(1,128)S(1)} async-done(((f32[16,1,5376]{2,1,0:T(1,128)}), f32[16,1,5376]{2,1,0:T(1,128)S(1)}, u32[]{:S(2)}, u32[]{:S(2)}) %all-to-all-start.2) | async-done | bytes 344096 | tf_op jit(solution)/shard_map/all_to_all | solution.py:98
  26.1 4.2 %all-to-all-start = ((f32[16,1,5376]{2,1,0:T(1,128)}), f32[16,1,5376]{2,1,0:T(1,128)}, u32[]{:S(2)}, u32[]{:S(2)}) async-start(f32[16,1,5376]{2,1,0:T(1,128)} %bitcast.5), calls=%async_computation | async-start | bytes 688128 | tf_op jit(solution)/shard_map/all_to_all | solution.py:97
  30.3 2.3 broadcast_in_dim.52
  32.6 192.7 %while.22 = (s32[]{:T(128)}, bf16[48,5376]{1,0:T(8,128)(2,1)}, f32[5376,64]{0,1:T(8,128)S(1)}, f32[64,5376]{1,0:T(8,128)}, bf16[8,48,5376]{2,1,0:T(8,128)(2,1)},...) while((s32[]{:T(128)}, bf16[48,5376]{1,0:T(8,128)(2,1)}, ...), condition=%wide.region_1.2_spmd.clone, body=%wide.region_0.1_spmd.clone.sunk | while | flops 168806416 | bytes 28440968 | solution.py:87
  39.9 9.6 %collective-permute-done = bf16[48,5376]{1,0:T(8,128)(2,1)} collective-permute-done((bf16[48,5376]{1,0:T(8,128)(2,1)}, bf16[48,5376]{1,0:T(8,128)(2,1)}, u32[]{:S(2)}, u32[]{:S(2)}) %collective-permute-start) | collective-permute-done | bytes 516128 | tf_op jit(solution)/shard_map/while/body/eval_jaxpr/ppermute | solution.py:16
  56.1 1.9 broadcast_select_fusion.2
  64.5 8.7 %collective-permute-done = bf16[48,5376]{1,0:T(8,128)(2,1)} collective-permute-done((bf16[48,5376]{1,0:T(8,128)(2,1)}, bf16[48,5376]{1,0:T(8,128)(2,1)}, u32[]{:S(2)}, u32[]{:S(2)}) %collective-permute-start) | collective-permute-done | bytes 516128 | tf_op jit(solution)/shard_map/while/body/eval_jaxpr/ppermute | solution.py:16
  79.8 1.9 broadcast_select_fusion.2
  88.1 7.9 %collective-permute-done = bf16[48,5376]{1,0:T(8,128)(2,1)} collective-permute-done((bf16[48,5376]{1,0:T(8,128)(2,1)}, bf16[48,5376]{1,0:T(8,128)(2,1)}, u32[]{:S(2)}, u32[]{:S(2)}) %collective-permute-start) | collective-permute-done | bytes 516128 | tf_op jit(solution)/shard_map/while/body/eval_jaxpr/ppermute | solution.py:16
  111.0 7.0 %collective-permute-done = bf16[48,5376]{1,0:T(8,128)(2,1)} collective-permute-done((bf16[48,5376]{1,0:T(8,128)(2,1)}, bf16[48,5376]{1,0:T(8,128)(2,1)}, u32[]{:S(2)}, u32[]{:S(2)}) %collective-permute-start) | collective-permute-done | bytes 516128 | tf_op jit(solution)/shard_map/while/body/eval_jaxpr/ppermute | solution.py:16
  124.6 1.9 broadcast_select_fusion.2
  132.9 6.2 %collective-permute-done = bf16[48,5376]{1,0:T(8,128)(2,1)} collective-permute-done((bf16[48,5376]{1,0:T(8,128)(2,1)}, bf16[48,5376]{1,0:T(8,128)(2,1)}, u32[]{:S(2)}, u32[]{:S(2)}) %collective-permute-start) | collective-permute-done | bytes 516128 | tf_op jit(solution)/shard_map/while/body/eval_jaxpr/ppermute | solution.py:16
  154.1 5.3 %collective-permute-done = bf16[48,5376]{1,0:T(8,128)(2,1)} collective-permute-done((bf16[48,5376]{1,0:T(8,128)(2,1)}, bf16[48,5376]{1,0:T(8,128)(2,1)}, u32[]{:S(2)}, u32[]{:S(2)}) %collective-permute-start) | collective-permute-done | bytes 516128 | tf_op jit(solution)/shard_map/while/body/eval_jaxpr/ppermute | solution.py:16
  174.4 4.8 %collective-permute-done = bf16[48,5376]{1,0:T(8,128)(2,1)} collective-permute-done((bf16[48,5376]{1,0:T(8,128)(2,1)}, bf16[48,5376]{1,0:T(8,128)(2,1)}, u32[]{:S(2)}, u32[]{:S(2)}) %collective-permute-start) | collective-permute-done | bytes 516128 | tf_op jit(solution)/shard_map/while/body/eval_jaxpr/ppermute | solution.py:16
  194.1 4.8 %collective-permute-done = bf16[48,5376]{1,0:T(8,128)(2,1)} collective-permute-done((bf16[48,5376]{1,0:T(8,128)(2,1)}, bf16[48,5376]{1,0:T(8,128)(2,1)}, u32[]{:S(2)}, u32[]{:S(2)}) %collective-permute-start) | collective-permute-done | bytes 516128 | tf_op jit(solution)/shard_map/while/body/eval_jaxpr/ppermute | solution.py:16
  213.9 4.8 %collective-permute-done = bf16[48,5376]{1,0:T(8,128)(2,1)} collective-permute-done((bf16[48,5376]{1,0:T(8,128)(2,1)}, bf16[48,5376]{1,0:T(8,128)(2,1)}, u32[]{:S(2)}, u32[]{:S(2)}) %collective-permute-start) | collective-permute-done | bytes 516128 | tf_op jit(solution)/shard_map/while/body/eval_jaxpr/ppermute | solution.py:16
  226.7 2.1 copy.18
  228.8 2.9 reshape.52
  234.0 5.3 %all-to-all-start.3 = ((f32[16,1,5376]{2,1,0:T(1,128)}), f32[16,1,5376]{2,1,0:T(1,128)S(1)}, u32[]{:S(2)}, u32[]{:S(2)}) async-start(f32[16,1,5376]{2,1,0:T(1,128)} %copy.19), calls=%async_computation.3 | async-start | bytes 688128 | tf_op jit(solution)/shard_map/all_to_all | solution.py:108
  247.4 3.2 all-to-all-done.3
  250.6 3.5 all-to-all-start.1
  254.3 15.2 %all-to-all-done.1 = f32[16,1,5376]{2,1,0:T(1,128)S(1)} async-done(((f32[16,1,5376]{2,1,0:T(1,128)}), f32[16,1,5376]{2,1,0:T(1,128)S(1)}, u32[]{:S(2)}, u32[]{:S(2)}) %all-to-all-start.1) | async-done | bytes 344096 | tf_op jit(solution)/shard_map/all_to_all | solution.py:107
  269.7 82.0 %all-reduce.2.cloned.1.call-done = f32[688128]{0:T(1024)} async-done(((f32[688128]{0:T(1024)}), f32[688128]{0:T(1024)}) %all-reduce.2.cloned.1.call-update) | async-done | bytes 2752528 | tf_op jit(solution)/shard_map/psum | solution.py:91
  (165 shorter events, 123.1 us)
Async XLA Ops:
  7.2 9.9 %copy-start.8 = (s32[1,16]{1,0:T(1,128)S(1)}, s32[1,16]{1,0:T(1,128)}, u32[]{:S(2)}) copy-start(s32[1,16]{1,0:T(1,128)} %param.20) | copy-start | bytes 196
  7.2 10.6 %copy-start.7 = (s32[1,8]{1,0:T(1,128)S(1)}, s32[1,8]{1,0:T(1,128)}, u32[]{:S(2)}) copy-start(s32[1,8]{1,0:T(1,128)} %param.19) | copy-start | bytes 100
  7.2 18.9 %all-to-all-start.2 = ((f32[16,1,5376]{2,1,0:T(1,128)}), f32[16,1,5376]{2,1,0:T(1,128)S(1)}, u32[]{:S(2)}, u32[]{:S(2)}) async-start(f32[16,1,5376]{2,1,0:T(1,128)} %bitcast.84), calls=%async_computation.2 | async-start | bytes 688128 | tf_op jit(solution)/shard_map/all_to_all | solution.py:98
  26.1 4.2 %copy-start.4 = (f32[16,1,5376]{2,1,0:T(1,128)}, f32[16,1,5376]{2,1,0:T(1,128)S(1)}, u32[]{:S(2)}) copy-start(f32[16,1,5376]{2,1,0:T(1,128)S(1)} %all-to-all-done.2) | copy-start | bytes 1032196
  26.1 207.9 %all-to-all-start = ((f32[16,1,5376]{2,1,0:T(1,128)}), f32[16,1,5376]{2,1,0:T(1,128)}, u32[]{:S(2)}, u32[]{:S(2)}) async-start(f32[16,1,5376]{2,1,0:T(1,128)} %bitcast.5), calls=%async_computation | async-start | bytes 688128 | tf_op jit(solution)/shard_map/all_to_all | solution.py:97
  30.3 2.3 copy-start.2
  30.3 2.3 copy-start.6
  33.4 16.1 %collective-permute-start = (bf16[48,5376]{1,0:T(8,128)(2,1)}, bf16[48,5376]{1,0:T(8,128)(2,1)}, u32[]{:S(2)}, u32[]{:S(2)}) collective-permute-start(bf16[48,5376]{1,0:T(8,128)(2,1)} %broadcast_select_fusion.2), channel_id=1, source_target_pairs={{16,0},{17,1},{18,2},{19,3},{20,4},{21,5},{22,6},{23,7},{24,8},{25... | collective-permute-start | bytes 1548296 | tf_op jit(solution)/shard_map/while/body/eval_jaxpr/ppermute | solution.py:16
  52.7 1.8 copy-start
  58.0 15.2 %collective-permute-start = (bf16[48,5376]{1,0:T(8,128)(2,1)}, bf16[48,5376]{1,0:T(8,128)(2,1)}, u32[]{:S(2)}, u32[]{:S(2)}) collective-permute-start(bf16[48,5376]{1,0:T(8,128)(2,1)} %broadcast_select_fusion.2), channel_id=1, source_target_pairs={{16,0},{17,1},{18,2},{19,3},{20,4},{21,5},{22,6},{23,7},{24,8},{25... | collective-permute-start | bytes 1548296 | tf_op jit(solution)/shard_map/while/body/eval_jaxpr/ppermute | solution.py:16
  76.4 1.8 copy-start
  81.7 14.4 %collective-permute-start = (bf16[48,5376]{1,0:T(8,128)(2,1)}, bf16[48,5376]{1,0:T(8,128)(2,1)}, u32[]{:S(2)}, u32[]{:S(2)}) collective-permute-start(bf16[48,5376]{1,0:T(8,128)(2,1)} %broadcast_select_fusion.2), channel_id=1, source_target_pairs={{16,0},{17,1},{18,2},{19,3},{20,4},{21,5},{22,6},{23,7},{24,8},{25... | collective-permute-start | bytes 1548296 | tf_op jit(solution)/shard_map/while/body/eval_jaxpr/ppermute | solution.py:16
  104.5 13.5 %collective-permute-start = (bf16[48,5376]{1,0:T(8,128)(2,1)}, bf16[48,5376]{1,0:T(8,128)(2,1)}, u32[]{:S(2)}, u32[]{:S(2)}) collective-permute-start(bf16[48,5376]{1,0:T(8,128)(2,1)} %broadcast_select_fusion.2), channel_id=1, source_target_pairs={{16,0},{17,1},{18,2},{19,3},{20,4},{21,5},{22,6},{23,7},{24,8},{25... | collective-permute-start | bytes 1548296 | tf_op jit(solution)/shard_map/while/body/eval_jaxpr/ppermute | solution.py:16
  126.4 12.7 %collective-permute-start = (bf16[48,5376]{1,0:T(8,128)(2,1)}, bf16[48,5376]{1,0:T(8,128)(2,1)}, u32[]{:S(2)}, u32[]{:S(2)}) collective-permute-start(bf16[48,5376]{1,0:T(8,128)(2,1)} %broadcast_select_fusion.2), channel_id=1, source_target_pairs={{16,0},{17,1},{18,2},{19,3},{20,4},{21,5},{22,6},{23,7},{24,8},{25... | collective-permute-start | bytes 1548296 | tf_op jit(solution)/shard_map/while/body/eval_jaxpr/ppermute | solution.py:16
  142.3 1.8 copy-start
  147.6 11.8 %collective-permute-start = (bf16[48,5376]{1,0:T(8,128)(2,1)}, bf16[48,5376]{1,0:T(8,128)(2,1)}, u32[]{:S(2)}, u32[]{:S(2)}) collective-permute-start(bf16[48,5376]{1,0:T(8,128)(2,1)} %broadcast_select_fusion.2), channel_id=1, source_target_pairs={{16,0},{17,1},{18,2},{19,3},{20,4},{21,5},{22,6},{23,7},{24,8},{25... | collective-permute-start | bytes 1548296 | tf_op jit(solution)/shard_map/while/body/eval_jaxpr/ppermute | solution.py:16
  167.9 11.3 %collective-permute-start = (bf16[48,5376]{1,0:T(8,128)(2,1)}, bf16[48,5376]{1,0:T(8,128)(2,1)}, u32[]{:S(2)}, u32[]{:S(2)}) collective-permute-start(bf16[48,5376]{1,0:T(8,128)(2,1)} %broadcast_select_fusion.2), channel_id=1, source_target_pairs={{16,0},{17,1},{18,2},{19,3},{20,4},{21,5},{22,6},{23,7},{24,8},{25... | collective-permute-start | bytes 1548296 | tf_op jit(solution)/shard_map/while/body/eval_jaxpr/ppermute | solution.py:16
  187.6 11.3 %collective-permute-start = (bf16[48,5376]{1,0:T(8,128)(2,1)}, bf16[48,5376]{1,0:T(8,128)(2,1)}, u32[]{:S(2)}, u32[]{:S(2)}) collective-permute-start(bf16[48,5376]{1,0:T(8,128)(2,1)} %broadcast_select_fusion.2), channel_id=1, source_target_pairs={{16,0},{17,1},{18,2},{19,3},{20,4},{21,5},{22,6},{23,7},{24,8},{25... | collective-permute-start | bytes 1548296 | tf_op jit(solution)/shard_map/while/body/eval_jaxpr/ppermute | solution.py:16
  207.4 11.3 %collective-permute-start = (bf16[48,5376]{1,0:T(8,128)(2,1)}, bf16[48,5376]{1,0:T(8,128)(2,1)}, u32[]{:S(2)}, u32[]{:S(2)}) collective-permute-start(bf16[48,5376]{1,0:T(8,128)(2,1)} %broadcast_select_fusion.2), channel_id=1, source_target_pairs={{16,0},{17,1},{18,2},{19,3},{20,4},{21,5},{22,6},{23,7},{24,8},{25... | collective-permute-start | bytes 1548296 | tf_op jit(solution)/shard_map/while/body/eval_jaxpr/ppermute | solution.py:16
  228.8 3.1 copy-start.5
  232.5 6.8 %copy-start.3 = (f32[344064]{0:T(1024)S(1)}, f32[344064]{0:T(1024)}, u32[]{:S(2)}) copy-start(f32[344064]{0:T(1024)} %reshape.52) | copy-start | bytes 4128772
  234.0 16.6 %all-to-all-start.3 = ((f32[16,1,5376]{2,1,0:T(1,128)}), f32[16,1,5376]{2,1,0:T(1,128)S(1)}, u32[]{:S(2)}, u32[]{:S(2)}) async-start(f32[16,1,5376]{2,1,0:T(1,128)} %copy.19), calls=%async_computation.3 | async-start | bytes 688128 | tf_op jit(solution)/shard_map/all_to_all | solution.py:108
  239.3 112.5 %all-reduce.2.cloned.1.call-start = ((), (), s32[]{:S(2)}) async-start(), calls=%async_computation.4 | async-start | bytes 5505024 | tf_op jit(solution)/shard_map/psum | solution.py:91
  250.6 18.9 %all-to-all-start.1 = ((f32[16,1,5376]{2,1,0:T(1,128)}), f32[16,1,5376]{2,1,0:T(1,128)S(1)}, u32[]{:S(2)}, u32[]{:S(2)}) async-start(f32[16,1,5376]{2,1,0:T(1,128)} %copy.17), calls=%async_computation.1 | async-start | bytes 688128 | tf_op jit(solution)/shard_map/all_to_all | solution.py:107
  (15 other events, 20.4 us)
Sparse Core Ops, SparseCore 0:
  243.7 108.0 all-reduce.1
where the time goes:
time: 363 us; the launch traced here: 360 us
  waiting for transfers between devices  168 us (46%)
  matrix products  51.1 us (14%)
  local copies, waits for them, and re-layouts  40.9 us (11%)
  other arithmetic  32.4 us (9%)
  starting transfers between devices  32.1 us (9%)
  loops' own time  19.1 us (5%)
  between operations  16.9 us (5%)
    psum x1, waiting for transfers between devices, per_device(): totals = lax.psum(partial_value, 'dp')  82 us
    ppermute x9, waiting for transfers between devices, passed_along(): lax.ppermute(value, axis, [(source, source + steps) for source in range(f...  59.2 us
    another operation x1, loops' own time, per_device(): lax.fori_loop(0, micro_count + sections - 1, drain_turn, start_state)  19.1 us
    while x9, other arithmetic  15.8 us
    dot_general x9, matrix products, drain_turn(): jnp.dot(section_input.T, pre_grad, preferred_element_type=jnp.float32)  15.7 us
    all_to_all x1, waiting for transfers between devices, per_device(): lax.all_to_all(first_out, 'dp', split_axis=0, concat_axis=0, tiled=True)  15.2 us
    dot_general x9, matrix products, drain_turn(): jnp.dot(pre_grad, weight_in.T, preferred_element_type=jnp.float32)  14.3 us
    dot_general x9, matrix products, drain_turn(): jnp.dot(section_input, weight_in, preferred_element_type=jnp.float32)  12.6 us
  transfers between devices with their start and end apart: 14, of which 13 were waited for; matrix products, arithmetic and copies ran while one was open for 31% of the time, Pallas kernels for 0%

commit v1 on v0

--- a/solution.py
+++ b/solution.py
@@ -88,7 +88,11 @@
         0, micro_count + sections - 1, drain_turn, start_state
     )
     partial_value = jnp.concatenate([grad_in.reshape(-1), grad_out.reshape(-1)])
-    totals = lax.psum(partial_value, "dp")
+    size = lax.axis_size("dp")
+    totals, hop = (partial_value, 1)
+    while hop < size:
+        totals = totals + lax.ppermute(totals, "dp", [(i, i ^ hop) for i in range(size)])
+        hop = 2 * hop
     grads = lax.dynamic_slice_in_dim(totals, new_block * block_len, block_len) / loss_scale
     old_count = owners_old.shape[0]
     piece_len = 2 * block_len // replicas

time: 363 us -> 503 us (1.39)
  waiting for transfers between devices: 168 us -> 316 us
  between operations: 16.9 us -> 3.47 us
    ppermute x0 -> x4, waiting for transfers between devices: none -> 126 us  [per_device(): lax.ppermute(totals, 'dp', [(i, i ^ hop) for i in range(size)])]
    all_to_all x1, waiting for transfers between devices: 0.01 us -> 115 us  [per_device(): lax.all_to_all(first_pieces, 'dp', split_axis=0, concat_axis=0, tiled=True)]
    psum x1 -> x0, waiting for transfers between devices: 82 us -> none  [per_device(): totals = lax.psum(partial_value, 'dp')]
    all_to_all x1, waiting for transfers between devices: 8.27 us -> 0.01 us  [per_device(): lax.all_to_all(second_pieces, 'dp', split_axis=0, concat_axis=0, tiled=True)]
    add x0 -> x3, other arithmetic: none -> 5.92 us  [per_device(): totals + lax.ppermute(totals, 'dp', [(i, i ^ hop) for i in range(size)])]
  transfers between devices with their start and end apart: 14 -> 17, of which waited for: 13 -> 15; matrix products, arithmetic and copies ran while one was open for 31% -> 8% of each run, Pallas kernels for 0% -> 0%
where the time goes in v1:
time: 503 us; the launch traced here: 500 us
  waiting for transfers between devices  316 us (63%)
  matrix products  51.1 us (10%)
  local copies, waits for them, and re-layouts  40.9 us (8%)
  other arithmetic  36.6 us (7%)
  starting transfers between devices  32.1 us (6%)
  loops' own time  19.4 us (4%)
    ppermute x4, waiting for transfers between devices, per_device(): lax.ppermute(totals, 'dp', [(i, i ^ hop) for i in range(size)])  126 us
    all_to_all x1, waiting for transfers between devices, per_device(): lax.all_to_all(first_pieces, 'dp', split_axis=0, concat_axis=0, tiled=True)  115 us
    ppermute x9, waiting for transfers between devices, passed_along(): lax.ppermute(value, axis, [(source, source + steps) for source in range(f...  58.6 us
    another operation x1, loops' own time, per_device(): lax.fori_loop(0, micro_count + sections - 1, drain_turn, start_state)  19.4 us
    while x9, other arithmetic  15.7 us
    dot_general x9, matrix products, drain_turn(): jnp.dot(section_input.T, pre_grad, preferred_element_type=jnp.float32)  15.7 us
    dot_general x9, matrix products, drain_turn(): jnp.dot(pre_grad, weight_in.T, preferred_element_type=jnp.float32)  14.3 us
    dot_general x9, matrix products, drain_turn(): jnp.dot(section_input, weight_in, preferred_element_type=jnp.float32)  12.6 us
  transfers between devices with their start and end apart: 17, of which 15 were waited for; matrix products, arithmetic and copies ran while one was open for 8% of the time, Pallas kernels for 0%

profile of v1, /device:TPU:0, one launch (start us, length us, event | category | flops | bytes accessed | tf_op | source)
XLA Modules:
  0.0 499.9 jit_solution(18273292959889319755)
XLA Ops:
  2.4 2.3 broadcast_in_dim.52
  4.7 192.6 %while.22 = (s32[]{:T(128)}, bf16[48,5376]{1,0:T(8,128)(2,1)}, f32[5376,64]{0,1:T(8,128)S(1)}, f32[64,5376]{1,0:T(8,128)}, bf16[8,48,5376]{2,1,0:T(8,128)(2,1)},...) while((s32[]{:T(128)}, bf16[48,5376]{1,0:T(8,128)(2,1)}, ...), condition=%wide.region_1.2_spmd.clone, body=%wide.region_0.1_spmd.clone.sunk | while | flops 168806416 | bytes 28440968 | solution.py:87
  12.1 9.8 %collective-permute-done = bf16[48,5376]{1,0:T(8,128)(2,1)} collective-permute-done((bf16[48,5376]{1,0:T(8,128)(2,1)}, bf16[48,5376]{1,0:T(8,128)(2,1)}, u32[]{:S(2)}, u32[]{:S(2)}) %collective-permute-start) | collective-permute-done | bytes 516128 | tf_op jit(solution)/shard_map/while/body/eval_jaxpr/ppermute | solution.py:16
  36.9 8.6 %collective-permute-done = bf16[48,5376]{1,0:T(8,128)(2,1)} collective-permute-done((bf16[48,5376]{1,0:T(8,128)(2,1)}, bf16[48,5376]{1,0:T(8,128)(2,1)}, u32[]{:S(2)}, u32[]{:S(2)}) %collective-permute-start) | collective-permute-done | bytes 516128 | tf_op jit(solution)/shard_map/while/body/eval_jaxpr/ppermute | solution.py:16
  60.5 7.8 %collective-permute-done = bf16[48,5376]{1,0:T(8,128)(2,1)} collective-permute-done((bf16[48,5376]{1,0:T(8,128)(2,1)}, bf16[48,5376]{1,0:T(8,128)(2,1)}, u32[]{:S(2)}, u32[]{:S(2)}) %collective-permute-start) | collective-permute-done | bytes 516128 | tf_op jit(solution)/shard_map/while/body/eval_jaxpr/ppermute | solution.py:16
  83.3 6.9 %collective-permute-done = bf16[48,5376]{1,0:T(8,128)(2,1)} collective-permute-done((bf16[48,5376]{1,0:T(8,128)(2,1)}, bf16[48,5376]{1,0:T(8,128)(2,1)}, u32[]{:S(2)}, u32[]{:S(2)}) %collective-permute-start) | collective-permute-done | bytes 516128 | tf_op jit(solution)/shard_map/while/body/eval_jaxpr/ppermute | solution.py:16
  105.2 6.0 %collective-permute-done = bf16[48,5376]{1,0:T(8,128)(2,1)} collective-permute-done((bf16[48,5376]{1,0:T(8,128)(2,1)}, bf16[48,5376]{1,0:T(8,128)(2,1)}, u32[]{:S(2)}, u32[]{:S(2)}) %collective-permute-start) | collective-permute-done | bytes 516128 | tf_op jit(solution)/shard_map/while/body/eval_jaxpr/ppermute | solution.py:16
  126.2 5.2 %collective-permute-done = bf16[48,5376]{1,0:T(8,128)(2,1)} collective-permute-done((bf16[48,5376]{1,0:T(8,128)(2,1)}, bf16[48,5376]{1,0:T(8,128)(2,1)}, u32[]{:S(2)}, u32[]{:S(2)}) %collective-permute-start) | collective-permute-done | bytes 516128 | tf_op jit(solution)/shard_map/while/body/eval_jaxpr/ppermute | solution.py:16
  146.4 4.7 collective-permute-done
  166.2 4.8 collective-permute-done
  185.9 4.7 collective-permute-done
  197.3 2.1 copy.18
  204.5 5.3 %collective-permute-done.1 = f32[688128]{0:T(1024)S(1)} collective-permute-done((f32[688128]{0:T(1024)}, f32[688128]{0:T(1024)S(1)}, u32[]{:S(2)}, u32[]{:S(2)}) %collective-permute-start.1) | collective-permute-done | bytes 2752544 | tf_op jit(solution)/shard_map/ppermute | solution.py:94
  209.8 2.1 add.125
  212.6 61.0 %collective-permute-done.2 = f32[688128]{0:T(1024)S(1)} collective-permute-done((f32[688128]{0:T(1024)S(1)}, f32[688128]{0:T(1024)S(1)}, u32[]{:S(2)}, u32[]{:S(2)}) %collective-permute-start.2) | collective-permute-done | bytes 2752544 | tf_op jit(solution)/shard_map/ppermute | solution.py:94
  274.7 4.8 all-to-all-start.2
  279.6 59.5 %collective-permute-done.3 = f32[688128]{0:T(1024)} collective-permute-done((f32[688128]{0:T(1024)S(1)}, f32[688128]{0:T(1024)}, u32[]{:S(2)}, u32[]{:S(2)}) %collective-permute-start.3) | collective-permute-done | bytes 2752544 | tf_op jit(solution)/shard_map/ppermute | solution.py:94
  339.1 3.6 add.127
  342.8 5.4 %all-to-all-start = ((f32[16,1,5376]{2,1,0:T(1,128)}), f32[16,1,5376]{2,1,0:T(1,128)S(1)}, u32[]{:S(2)}, u32[]{:S(2)}) async-start(f32[16,1,5376]{2,1,0:T(1,128)} %bitcast.5), calls=%async_computation | async-start | bytes 688128 | tf_op jit(solution)/shard_map/all_to_all | solution.py:101
  351.9 114.8 %all-to-all-done = f32[16,1,5376]{2,1,0:T(1,128)S(1)} async-done(((f32[16,1,5376]{2,1,0:T(1,128)}), f32[16,1,5376]{2,1,0:T(1,128)S(1)}, u32[]{:S(2)}, u32[]{:S(2)}) %all-to-all-start) | async-done | bytes 344096 | tf_op jit(solution)/shard_map/all_to_all | solution.py:101
  466.7 5.0 %all-to-all-start.3 = ((f32[16,1,5376]{2,1,0:T(1,128)}), f32[16,1,5376]{2,1,0:T(1,128)S(1)}, u32[]{:S(2)}, u32[]{:S(2)}) async-start(f32[16,1,5376]{2,1,0:T(1,128)} %copy.19), calls=%async_computation.3 | async-start | bytes 688128 | tf_op jit(solution)/shard_map/all_to_all | solution.py:112
  477.0 6.0 %all-to-all-done.3 = f32[16,1,5376]{2,1,0:T(1,128)S(1)} async-done(((f32[16,1,5376]{2,1,0:T(1,128)}), f32[16,1,5376]{2,1,0:T(1,128)S(1)}, u32[]{:S(2)}, u32[]{:S(2)}) %all-to-all-start.3) | async-done | bytes 344096 | tf_op jit(solution)/shard_map/all_to_all | solution.py:112
  483.0 3.5 all-to-all-start.1
  486.8 11.1 %all-to-all-done.1 = f32[16,1,5376]{2,1,0:T(1,128)S(1)} async-done(((f32[16,1,5376]{2,1,0:T(1,128)}), f32[16,1,5376]{2,1,0:T(1,128)S(1)}, u32[]{:S(2)}, u32[]{:S(2)}) %all-to-all-start.1) | async-done | bytes 344096 | tf_op jit(solution)/shard_map/all_to_all | solution.py:111
  (170 shorter events, 131.9 us)
Async XLA Ops:
  2.4 2.3 copy-start.3
  2.4 2.3 copy-start.4
  5.5 16.3 %collective-permute-start = (bf16[48,5376]{1,0:T(8,128)(2,1)}, bf16[48,5376]{1,0:T(8,128)(2,1)}, u32[]{:S(2)}, u32[]{:S(2)}) collective-permute-start(bf16[48,5376]{1,0:T(8,128)(2,1)} %broadcast_select_fusion.2), channel_id=1, source_target_pairs={{16,0},{17,1},{18,2},{19,3},{20,4},{21,5},{22,6},{23,7},{24,8},{25... | collective-permute-start | bytes 1548296 | tf_op jit(solution)/shard_map/while/body/eval_jaxpr/ppermute | solution.py:16
  30.3 15.2 %collective-permute-start = (bf16[48,5376]{1,0:T(8,128)(2,1)}, bf16[48,5376]{1,0:T(8,128)(2,1)}, u32[]{:S(2)}, u32[]{:S(2)}) collective-permute-start(bf16[48,5376]{1,0:T(8,128)(2,1)} %broadcast_select_fusion.2), channel_id=1, source_target_pairs={{16,0},{17,1},{18,2},{19,3},{20,4},{21,5},{22,6},{23,7},{24,8},{25... | collective-permute-start | bytes 1548296 | tf_op jit(solution)/shard_map/while/body/eval_jaxpr/ppermute | solution.py:16
  48.7 1.8 copy-start
  54.0 14.3 %collective-permute-start = (bf16[48,5376]{1,0:T(8,128)(2,1)}, bf16[48,5376]{1,0:T(8,128)(2,1)}, u32[]{:S(2)}, u32[]{:S(2)}) collective-permute-start(bf16[48,5376]{1,0:T(8,128)(2,1)} %broadcast_select_fusion.2), channel_id=1, source_target_pairs={{16,0},{17,1},{18,2},{19,3},{20,4},{21,5},{22,6},{23,7},{24,8},{25... | collective-permute-start | bytes 1548296 | tf_op jit(solution)/shard_map/while/body/eval_jaxpr/ppermute | solution.py:16
  76.7 13.4 %collective-permute-start = (bf16[48,5376]{1,0:T(8,128)(2,1)}, bf16[48,5376]{1,0:T(8,128)(2,1)}, u32[]{:S(2)}, u32[]{:S(2)}) collective-permute-start(bf16[48,5376]{1,0:T(8,128)(2,1)} %broadcast_select_fusion.2), channel_id=1, source_target_pairs={{16,0},{17,1},{18,2},{19,3},{20,4},{21,5},{22,6},{23,7},{24,8},{25... | collective-permute-start | bytes 1548296 | tf_op jit(solution)/shard_map/while/body/eval_jaxpr/ppermute | solution.py:16
  98.6 12.6 %collective-permute-start = (bf16[48,5376]{1,0:T(8,128)(2,1)}, bf16[48,5376]{1,0:T(8,128)(2,1)}, u32[]{:S(2)}, u32[]{:S(2)}) collective-permute-start(bf16[48,5376]{1,0:T(8,128)(2,1)} %broadcast_select_fusion.2), channel_id=1, source_target_pairs={{16,0},{17,1},{18,2},{19,3},{20,4},{21,5},{22,6},{23,7},{24,8},{25... | collective-permute-start | bytes 1548296 | tf_op jit(solution)/shard_map/while/body/eval_jaxpr/ppermute | solution.py:16
  114.4 1.8 copy-start
  119.7 11.7 %collective-permute-start = (bf16[48,5376]{1,0:T(8,128)(2,1)}, bf16[48,5376]{1,0:T(8,128)(2,1)}, u32[]{:S(2)}, u32[]{:S(2)}) collective-permute-start(bf16[48,5376]{1,0:T(8,128)(2,1)} %broadcast_select_fusion.2), channel_id=1, source_target_pairs={{16,0},{17,1},{18,2},{19,3},{20,4},{21,5},{22,6},{23,7},{24,8},{25... | collective-permute-start | bytes 1548296 | tf_op jit(solution)/shard_map/while/body/eval_jaxpr/ppermute | solution.py:16
  139.9 11.3 %collective-permute-start = (bf16[48,5376]{1,0:T(8,128)(2,1)}, bf16[48,5376]{1,0:T(8,128)(2,1)}, u32[]{:S(2)}, u32[]{:S(2)}) collective-permute-start(bf16[48,5376]{1,0:T(8,128)(2,1)} %broadcast_select_fusion.2), channel_id=1, source_target_pairs={{16,0},{17,1},{18,2},{19,3},{20,4},{21,5},{22,6},{23,7},{24,8},{25... | collective-permute-start | bytes 1548296 | tf_op jit(solution)/shard_map/while/body/eval_jaxpr/ppermute | solution.py:16
  159.6 11.3 %collective-permute-start = (bf16[48,5376]{1,0:T(8,128)(2,1)}, bf16[48,5376]{1,0:T(8,128)(2,1)}, u32[]{:S(2)}, u32[]{:S(2)}) collective-permute-start(bf16[48,5376]{1,0:T(8,128)(2,1)} %broadcast_select_fusion.2), channel_id=1, source_target_pairs={{16,0},{17,1},{18,2},{19,3},{20,4},{21,5},{22,6},{23,7},{24,8},{25... | collective-permute-start | bytes 1548296 | tf_op jit(solution)/shard_map/while/body/eval_jaxpr/ppermute | solution.py:16
  179.4 11.3 %collective-permute-start = (bf16[48,5376]{1,0:T(8,128)(2,1)}, bf16[48,5376]{1,0:T(8,128)(2,1)}, u32[]{:S(2)}, u32[]{:S(2)}) collective-permute-start(bf16[48,5376]{1,0:T(8,128)(2,1)} %broadcast_select_fusion.2), channel_id=1, source_target_pairs={{16,0},{17,1},{18,2},{19,3},{20,4},{21,5},{22,6},{23,7},{24,8},{25... | collective-permute-start | bytes 1548296 | tf_op jit(solution)/shard_map/while/body/eval_jaxpr/ppermute | solution.py:16
  201.4 1.8 copy-start.2
  204.5 5.3 %collective-permute-start.1 = (f32[688128]{0:T(1024)}, f32[688128]{0:T(1024)S(1)}, u32[]{:S(2)}, u32[]{:S(2)}) collective-permute-start(f32[688128]{0:T(1024)} %constant_dynamic-update-slice_fusion), channel_id=1, source_target_pairs={{0,1},{1,0},{2,3},{3,2},{4,5},{5,4},{6,7},{7,6},{8,9},{9,8},{10,11... | collective-permute-start | bytes 8257544 | tf_op jit(solution)/shard_map/ppermute | solution.py:94
  211.9 61.8 %collective-permute-start.2 = (f32[688128]{0:T(1024)S(1)}, f32[688128]{0:T(1024)S(1)}, u32[]{:S(2)}, u32[]{:S(2)}) collective-permute-start(f32[688128]{0:T(1024)S(1)} %add.125), channel_id=1, source_target_pairs={{0,2},{1,3},{2,0},{3,1},{4,6},{5,7},{6,4},{7,5},{8,10},{9,11},{10,... | collective-permute-start | bytes 8257544 | tf_op jit(solution)/shard_map/ppermute | solution.py:94
  273.9 65.2 %collective-permute-start.3 = (f32[688128]{0:T(1024)S(1)}, f32[688128]{0:T(1024)}, u32[]{:S(2)}, u32[]{:S(2)}) collective-permute-start(f32[688128]{0:T(1024)S(1)} %add.126), channel_id=1, source_target_pairs={{0,4},{1,5},{2,6},{3,7},{4,0},{5,1},{6,2},{7,3},{8,12},{9,13},{10,... | collective-permute-start | bytes 8257544 | tf_op jit(solution)/shard_map/ppermute | solution.py:94
  274.7 68.1 %all-to-all-start.2 = ((f32[16,1,5376]{2,1,0:T(1,128)}), f32[16,1,5376]{2,1,0:T(1,128)S(1)}, u32[]{:S(2)}, u32[]{:S(2)}) async-start(f32[16,1,5376]{2,1,0:T(1,128)} %bitcast.9), calls=%async_computation.2 | async-start | bytes 688128 | tf_op jit(solution)/shard_map/all_to_all | solution.py:102
  279.6 68.7 %copy-start.5 = (s32[1,8]{1,0:T(1,128)S(1)}, s32[1,8]{1,0:T(1,128)}, u32[]{:S(2)}) copy-start(s32[1,8]{1,0:T(1,128)} %param.19) | copy-start | bytes 100
  279.6 69.2 %copy-start.6 = (s32[1,16]{1,0:T(1,128)S(1)}, s32[1,16]{1,0:T(1,128)}, u32[]{:S(2)}) copy-start(s32[1,16]{1,0:T(1,128)} %param.20) | copy-start | bytes 196
  342.7 155.4 %collective-permute-start.4 = (f32[688128]{0:T(1024)}, f32[688128]{0:T(1024)}, u32[]{:S(2)}, u32[]{:S(2)}) collective-permute-start(f32[688128]{0:T(1024)} %add.127), channel_id=1, source_target_pairs={{0,8},{1,9},{2,10},{3,11},{4,12},{5,13},{6,14},{7,15},{8,0},{9,1},... | collective-permute-start | bytes 8257544 | tf_op jit(solution)/shard_map/ppermute | solution.py:94
  342.8 123.8 %all-to-all-start = ((f32[16,1,5376]{2,1,0:T(1,128)}), f32[16,1,5376]{2,1,0:T(1,128)S(1)}, u32[]{:S(2)}, u32[]{:S(2)}) async-start(f32[16,1,5376]{2,1,0:T(1,128)} %bitcast.5), calls=%async_computation | async-start | bytes 688128 | tf_op jit(solution)/shard_map/all_to_all | solution.py:101
  466.7 16.4 %all-to-all-start.3 = ((f32[16,1,5376]{2,1,0:T(1,128)}), f32[16,1,5376]{2,1,0:T(1,128)S(1)}, u32[]{:S(2)}, u32[]{:S(2)}) async-start(f32[16,1,5376]{2,1,0:T(1,128)} %copy.19), calls=%async_computation.3 | async-start | bytes 688128 | tf_op jit(solution)/shard_map/all_to_all | solution.py:112
  483.0 14.8 %all-to-all-start.1 = ((f32[16,1,5376]{2,1,0:T(1,128)}), f32[16,1,5376]{2,1,0:T(1,128)S(1)}, u32[]{:S(2)}, u32[]{:S(2)}) async-start(f32[16,1,5376]{2,1,0:T(1,128)} %copy.17), calls=%async_computation.1 | async-start | bytes 688128 | tf_op jit(solution)/shard_map/all_to_all | solution.py:111
  (16 other events, 22.3 us)
